TPU v7x, 128 devices: a whole 4x4x4 slice. The times are simulated.
128 devices in a mesh: gx: 16 (over z, y_hi, core), gy: 8 (over y_lo, x).
Axes of the slice: x: 4, y: 4 (y_hi: 2, y_lo: 2; y = y_hi * 2 + y_lo), z: 4, core: 2. Of those that a mesh axis runs over, the one named last changes fastest.
Arguments:
- density: float32 [256, 256, 256], P('gx', 'gy'), may hold values from 0.05 to 2
Outputs:
- potential: float32 [256, 256, 256], P('gx', 'gy')
- energy: float32 [], replicated
All inputs are finite; a program needn't handle non-finite values.
Results may differ from a plain program's by a relative error of at most 0.00005.
Values sent between devices are 32-bit elements.
No kernel may reach another device: no remote copies, remote signals or barrier semaphores. Data moves between devices by JAX's collectives and lax.ppermute only.
A program may use at most 64 MiB of HBM per device.

v0:
```python
import functools
import math

import jax
import jax.numpy as jnp
import numpy as np
from jax import lax
from jax.experimental import pallas as pl
from jax.experimental.pallas import tpu as pltpu
from jax.sharding import PartitionSpec as P

AXES = ("gx", "gy")
LANES = 128
VIEW = 8
highest = lax.Precision.HIGHEST

pbe_kappa = 0.804
pbe_mu = 0.2195149727645171
pbe_beta = 0.06672455060314922
pbe_gamma = 0.031090690869654894
pw_coef = 0.0310907
pw_alpha = 0.2137
pw_first = 7.5957
pw_second = 3.5876
pw_third = 1.6382
pw_fourth = 0.49294

fermi_scale = (3.0 * math.pi**2) ** (1.0 / 3.0)
exch_scale = 0.75 * fermi_scale / math.pi
s_scale = 1.0 / (4.0 * fermi_scale**2)
t_scale = math.pi / (16.0 * fermi_scale)
rs_scale = (3.0 / (4.0 * math.pi)) ** (1.0 / 3.0)
beta_gamma = pbe_beta / pbe_gamma


def deriv_matrix(count):
    index = np.arange(count)
    signed = np.where(index < count // 2, index, index - count)
    signed = np.where(index == count // 2, 0, signed)
    waves = signed * (2.0 * math.pi / count)
    phase = (index[:, None] * index[None, :] % count) * (2.0 * math.pi / count)
    cosine, sine = np.cos(phase), np.sin(phase)
    return ((cosine * waves) @ sine - (sine * waves) @ cosine) / count


def mul(left, right):
    return jnp.dot(left, right, precision=highest, preferred_element_type=jnp.float32)


def pbe(n, g):
    v = jnp.exp2(jnp.log2(n) * (-1.0 / 3.0))
    v = v * (4.0 / 3.0 - (1.0 / 3.0) * n * v * v * v)
    v2 = v * v
    v4 = v2 * v2
    u = n * v2
    g4 = g * v4
    s2 = s_scale * g4 * v4
    t2 = t_scale * g4 * v2 * v
    damp = 1.0 / (1.0 + (pbe_mu / pbe_kappa) * s2)
    ex = -exch_scale * u
    fx = 1.0 + pbe_kappa - pbe_kappa * damp
    slope = pbe_mu * damp * damp
    rs = rs_scale * v
    root = jnp.sqrt(rs)
    series = (2.0 * pw_coef) * root * (
        pw_first + root * (pw_second + root * (pw_third + root * pw_fourth))
    )
    dseries = (2.0 * pw_coef) * root * (
        0.5 * pw_first + root * (pw_second + root * (1.5 * pw_third + root * (2.0 * pw_fourth)))
    )
    inverse = 1.0 / series
    logarithm = jnp.log(1.0 + inverse)
    front = (-2.0 * pw_coef) * (1.0 + pw_alpha * rs)
    ec = front * logarithm
    rs_dec = (-2.0 * pw_coef * pw_alpha) * rs * logarithm - front * dseries * inverse / (
        1.0 + series
    )
    n_dec = (-1.0 / 3.0) * rs_dec
    below = 1.0 / (jnp.exp(ec * (-1.0 / pbe_gamma)) - 1.0)
    factor = beta_gamma * below
    n_dfactor = factor * (1.0 + below) * (1.0 / pbe_gamma) * n_dec
    y = factor * t2
    base = 1.0 + y + y * y
    top = base + beta_gamma * t2 * (1.0 + y)
    both = 1.0 / (base * top)
    h = pbe_gamma * jnp.log(top * top * both)
    energy = ex * fx + ec + h
    d_grad = v4 * (
        (-exch_scale * s_scale) * slope + (pbe_beta * t_scale) * (1.0 + 2.0 * y) * both
    )
    n_dh = pbe_beta * both * (
        (-7.0 / 3.0) * t2 * (1.0 + 2.0 * y) - t2 * t2 * y * (2.0 + y) * n_dfactor
    )
    d_dens = energy + ex * ((1.0 / 3.0) * fx - (8.0 / 3.0) * slope * s2) + n_dec + n_dh
    return n * energy, d_dens, d_grad


def quarter_swap(parts):
    quarter = lax.broadcasted_iota(jnp.int32, parts[0].shape, parts[0].ndim - 1) // 32
    for bit in (1, 2):
        upper = (quarter & bit) != 0
        swapped = list(parts)
        for low in range(4):
            if low & bit:
                continue
            high = low | bit
            first, second = parts[low], parts[high]
            axis = first.ndim - 1
            swapped[low] = jnp.where(upper, pltpu.roll(second, 32 * bit, axis), first)
            swapped[high] = jnp.where(upper, second, pltpu.roll(first, LANES - 32 * bit, axis))
        parts = swapped
    return parts


def first_kernel(density_ref, deriv_ref, send_ref):
    lines = density_ref[...].reshape(-1, density_ref.shape[-1])
    turned = lines.T
    slopes = mul(deriv_ref[...], turned)
    rows = 2 * VIEW
    for field, values in enumerate((turned, slopes)):
        for plane in range(2):
            for part in range(4):
                send_ref[pl.ds(VIEW * field + 4 * plane + part, LANES, stride=rows), :] = values[
                    LANES * plane : LANES * (plane + 1), LANES * part : LANES * (part + 1)
                ]


def middle_kernel(
    got_ref, deriv_x_ref, deriv_y_ref, send_ref, dens_ref, grad_z_ref, grad_x_ref, grad_y_ref
):
    rows = 2 * VIEW
    for a in range(16):
        for field, ref in enumerate((dens_ref, grad_z_ref)):
            for half in range(2):
                parts = []
                for quarter in range(4):
                    start = ((a * 2 + half) * 4 + quarter) * rows + VIEW * field
                    parts.append(got_ref[start : start + VIEW, :])
                for quarter, part in enumerate(quarter_swap(parts)):
                    start = (a * 4 + quarter) * VIEW
                    ref[start : start + VIEW, LANES * half : LANES * (half + 1)] = part
    grad_x_ref[...] = mul(deriv_x_ref[...], dens_ref[...])
    grad_y_ref[...] = mul(dens_ref[...], deriv_y_ref[...])

    def evaluate(step, total):
        block = pl.ds(pl.multiple_of(step * 32, 32), 32)
        n = dens_ref[block, :]
        gx, gy, gz = grad_x_ref[block, :], grad_y_ref[block, :], grad_z_ref[block, :]
        f, d_dens, d_grad = pbe(n, gx * gx + gy * gy + gz * gz)
        twice = 2.0 * d_grad
        grad_x_ref[block, :] = twice * gx
        grad_y_ref[block, :] = twice * gy
        grad_z_ref[block, :] = twice * gz
        dens_ref[block, :] = d_dens
        return total + f

    total = lax.fori_loop(0, 16, evaluate, jnp.zeros((32, 256), jnp.float32))
    dens_ref[...] = (
        dens_ref[...]
        - mul(deriv_x_ref[...], grad_x_ref[...])
        - mul(grad_y_ref[...], deriv_y_ref[...])
    )
    for a in range(16):
        for field, ref in enumerate((dens_ref, grad_z_ref)):
            for half in range(2):
                parts = []
                for quarter in range(4):
                    start = (a * 4 + quarter) * VIEW
                    parts.append(ref[start : start + VIEW, LANES * half : LANES * (half + 1)])
                for quarter, part in enumerate(quarter_swap(parts)):
                    start = ((a * 2 + half) * 4 + quarter) * (rows + 1) + VIEW * field
                    send_ref[start : start + VIEW, :] = part
    summed = jnp.sum(total[:, :LANES] + total[:, LANES:], axis=0, keepdims=True)
    send_ref[pl.ds(rows, LANES, stride=rows + 1), :] = jnp.broadcast_to(summed, (LANES, LANES))


def last_kernel(cells, got_ref, deriv_ref, potential_ref, energy_ref):
    rows = 2 * VIEW + 1

    def gather(field):
        return jnp.concatenate(
            [
                jnp.concatenate(
                    [
                        got_ref[pl.ds(VIEW * field + 4 * plane + part, LANES, stride=rows), :]
                        for part in range(4)
                    ],
                    axis=1,
                )
                for plane in range(2)
            ],
            axis=0,
        )

    turned = gather(0) - mul(deriv_ref[...], gather(1))
    potential_ref[...] = turned.T.reshape(potential_ref.shape)
    energy_ref[0, 0] = jnp.sum(got_ref[pl.ds(rows - 1, LANES, stride=rows), :]) / cells


def in_vmem(count):
    return [pl.BlockSpec(memory_space=pltpu.VMEM)] * count


def exchange(values):
    return lax.all_to_all(values, AXES, split_axis=0, concat_axis=0, tiled=True)


def body(cells, density):
    count = density.shape[-1]
    deriv = deriv_matrix(count)
    row = np.arange(2 * count)
    plane = (row // 4) % 2
    cell = 16 * (row // 32) + 4 * (row % 4) + (row // 8) % 4
    double = np.where(plane[:, None] == plane[None, :], deriv[cell[:, None], cell[None, :]], 0.0)
    deriv_z = jnp.asarray(deriv, jnp.float32)
    deriv_y = jnp.asarray(deriv.T, jnp.float32)
    deriv_x = jnp.asarray(double, jnp.float32)

    send = pl.pallas_call(
        first_kernel,
        out_shape=jax.ShapeDtypeStruct((2048, LANES), jnp.float32),
        in_specs=in_vmem(2),
        out_specs=pl.BlockSpec(memory_space=pltpu.VMEM),
    )(density, deriv_z)
    got = exchange(send.reshape(LANES, 16, LANES)).reshape(2048, LANES)
    send = pl.pallas_call(
        middle_kernel,
        out_shape=jax.ShapeDtypeStruct((17 * LANES, LANES), jnp.float32),
        in_specs=in_vmem(3),
        out_specs=pl.BlockSpec(memory_space=pltpu.VMEM),
        scratch_shapes=[pltpu.VMEM((512, 256), jnp.float32)] * 4,
    )(got, deriv_x, deriv_y)
    got = exchange(send.reshape(LANES, 1, 17 * LANES)).reshape(17 * LANES, LANES)
    potential, energy = pl.pallas_call(
        functools.partial(last_kernel, float(cells)),
        out_shape=(
            jax.ShapeDtypeStruct(density.shape, jnp.float32),
            jax.ShapeDtypeStruct((1, 1), jnp.float32),
        ),
        in_specs=in_vmem(2),
        out_specs=(
            pl.BlockSpec(memory_space=pltpu.VMEM),
            pl.BlockSpec(memory_space=pltpu.SMEM),
        ),
    )(got, deriv_z)
    return potential, energy.reshape(())


def solution(mesh):
    return jax.shard_map(
        functools.partial(body, 256**3),
        mesh=mesh,
        in_specs=(P("gx", "gy", None),),
        out_specs=(P("gx", "gy", None), P()),
        check_vma=False,
    )
```

profile of v0, /device:TPU:1, one launch (start us, length us, event | category | flops | bytes accessed | tf_op | source)
XLA Modules:
  0.0 72.4 jit_solution(14413891858676972909)
XLA Ops:
  0.6 3.1 %shard_map.59 = f32[2048,128]{1,0:T(8,128)} custom-call(f32[16,32,256]{2,1,0:T(8,128)} %density_ref.1, f32[256,256]{1,0:T(8,128)} %constant.6.clone.deriv_ref), custom_call_target="tpu_custom_call" | custom-call | tf_op jit(solution)/shard_map/pallas_call | solution.py:219
  3.7 31.0 %all_to_all.10 = f32[128,16,128]{2,1,0:T(8,128)} all-to-all(f32[128,16,128]{2,1,0:T(8,128)} %bitcast.7), channel_id=1, replica_groups=mesh['gx'=16,'gy'=8] {'gx','gy'}, dimensions={0} | all-to-all | bytes 2097152 | tf_op jit(solution)/shard_map/all_to_all | solution.py:205
  34.7 9.5 %shard_map.60 = f32[2176,128]{1,0:T(8,128)} custom-call(f32[2048,128]{1,0:T(8,128)} %bitcast.8, f32[512,512]{1,0:T(8,128)} %constant.8.clone.deriv_x_ref, f32[256,256]{1,0:T(8,128)} %constant.7.clone.deriv_y_ref), custom_call_target="tpu_custom_call" | custom-call | tf_op jit(solution)/shard_map/pallas_call | solution.py:226
  44.2 25.4 %all_to_all.11 = f32[128,1,2176]{2,1,0:T(1,128)} all-to-all(f32[128,1,2176]{2,1,0:T(1,128)} %bitcast.6), channel_id=1, replica_groups=mesh['gx'=16,'gy'=8] {'gx','gy'}, dimensions={0} | all-to-all | bytes 2228224 | tf_op jit(solution)/shard_map/all_to_all | solution.py:205
  69.5 2.9 %shard_map.61 = (f32[16,32,256]{2,1,0:T(8,128)}, f32[1,1]{1,0:T(1,128)}) custom-call(f32[2176,128]{1,0:T(8,128)} %bitcast.5, f32[256,256]{1,0:T(8,128)} %constant.6.clone.deriv_ref), custom_call_target="tpu_custom_call" | custom-call | tf_op jit(solution)/shard_map/pallas_call | solution.py:234
where the time goes:
time: 72.7 us; the launch traced here: 72.4 us
  blocking collectives  56.4 us (78%)
  Pallas kernels  15.4 us (21%)
    all_to_all x2, blocking collectives, exchange(): return lax.all_to_all(values, AXES, split_axis=0, concat_axis=0, tiled=True)  56.4 us
    pallas_call x1, Pallas kernels, body(): pl.pallas_call(middle_kernel, out_shape=jax.ShapeDtypeStruct((17 * LANES,...  9.49 us
    pallas_call x1, Pallas kernels, body(): pl.pallas_call(first_kernel, out_shape=jax.ShapeDtypeStruct((2048, LANES)...  3.05 us
    pallas_call x1, Pallas kernels, body(): pl.pallas_call(functools.partial(last_kernel, float(cells)), out_shape=(j...  2.89 us

commit v1 on v0

v1 whole, which is shorter than its diff:
```python
import functools
import math

import jax
import jax.numpy as jnp
import numpy as np
from jax import lax
from jax.experimental import pallas as pl
from jax.experimental.pallas import tpu as pltpu
from jax.sharding import PartitionSpec as P

AXES = ("gx", "gy")
LANES = 128
VIEW = 8
GROUP = 4
BLOCK = 32

pbe_kappa = 0.804
pbe_mu = 0.2195149727645171
pbe_beta = 0.06672455060314922
pbe_gamma = 0.031090690869654894
pw_coef = 0.0310907
pw_alpha = 0.2137
pw_first = 7.5957
pw_second = 3.5876
pw_third = 1.6382
pw_fourth = 0.49294

fermi_scale = (3.0 * math.pi**2) ** (1.0 / 3.0)
exch_scale = 0.75 * fermi_scale / math.pi
s_scale = 1.0 / (4.0 * fermi_scale**2)
t_scale = math.pi / (16.0 * fermi_scale)
rs_scale = (3.0 / (4.0 * math.pi)) ** (1.0 / 3.0)
root_slope = -1.0 / (6.0 * math.log(2.0))
root_shift = 0.5 * math.log2(rs_scale)
damping_scale = pbe_mu / pbe_kappa * s_scale / rs_scale**8
tau_scale = pbe_beta / pbe_gamma * t_scale / rs_scale**7
slope_scale = -2.0 * exch_scale * s_scale * pbe_mu / rs_scale**4
weight_scale = 2.0 * pbe_beta * t_scale / rs_scale**4
pw = [2.0 * pw_coef * factor for factor in (pw_first, pw_second, pw_third, pw_fourth)]


def deriv_matrix(count):
    index = np.arange(count)
    signed = np.where(index < count // 2, index, index - count)
    signed = np.where(index == count // 2, 0, signed)
    waves = signed * (2.0 * math.pi / count)
    phase = (index[:, None] * index[None, :] % count) * (2.0 * math.pi / count)
    cosine, sine = np.cos(phase), np.sin(phase)
    return ((cosine * waves) @ sine - (sine * waves) @ cosine) / count


def halves(values):
    high = values.astype(jnp.bfloat16)
    return high, (values - high.astype(jnp.float32)).astype(jnp.bfloat16)


def mul(left, right):
    def dot(first, second):
        return jnp.dot(first, second, preferred_element_type=jnp.float32)

    return dot(left[0], right[0]) + dot(left[1], right[0]) + dot(left[0], right[1])


def pbe(n, g):
    root = jnp.exp2(jnp.log(n) * root_slope + root_shift)
    rs = root * root
    rs2 = rs * rs
    rs4 = rs2 * rs2
    scaled = g * rs4
    damping = 1.0 + damping_scale * (scaled * rs4)
    tau = tau_scale * (scaled * (rs2 * rs))
    ex = (-exch_scale / rs_scale**2) * (n * rs2)
    series = root * (pw[0] + root * (pw[1] + root * (pw[2] + root * pw[3])))
    third = root * (
        pw[0] / 6 + root * (pw[1] / 3 + root * (pw[2] / 2 + root * (pw[3] / 1.5)))
    )
    outer = 1.0 + series
    product = series * outer
    inverse = 1.0 / (product * damping)
    damp = product * inverse
    fraction = damping * inverse
    logarithm = jnp.log(1.0 + outer * fraction)
    curved = (-2.0 * pw_coef * pw_alpha) * rs
    front = curved - 2.0 * pw_coef
    ec = front * logarithm
    n_dec = front * (third * fraction) - (curved * (1.0 / 3.0)) * logarithm
    grown = jnp.exp2(ec * (-1.0 / (pbe_gamma * math.log(2.0))))
    m = grown - 1.0
    m2 = m * m
    cross = tau * m
    tau2 = tau * tau
    near = m + tau
    base = m2 + cross + tau2
    top = base + cross * near
    both = 1.0 / (base * top)
    rest = ec + pbe_gamma * jnp.log(top * (top * both))
    damp2 = damp * damp
    energy = ex * ((1.0 + pbe_kappa) - pbe_kappa * damp) + rest
    weight = (near + tau) * (m2 * m)
    twice = rs4 * (slope_scale * damp2 + (weight_scale * weight) * both)
    n_dh = (tau * both) * (
        (-7.0 / 3.0 * pbe_gamma) * weight - tau2 * ((near + m) * (grown * n_dec))
    )
    d_dens = (
        ex
        * (
            (4.0 / 3.0) * (1.0 + pbe_kappa)
            + damp * ((-4.0 * pbe_kappa) + (8.0 / 3.0 * pbe_kappa) * damp)
        )
        + (rest + n_dec)
        + n_dh
    )
    return n * energy, d_dens, twice


def mix(parts, odd, upper):
    pairs = [jnp.where(odd, parts[(1 - t) % 4], parts[-t % 4]) for t in range(4)]
    return [jnp.where(upper, pairs[(t + 2) % 4], pairs[t]) for t in range(4)]


def swap_rows(first, second, below):
    return (
        jnp.where(below, pltpu.roll(second, 4, 0), first),
        jnp.where(below, second, pltpu.roll(first, 4, 0)),
    )


def masks():
    lane = lax.broadcasted_iota(jnp.int32, (VIEW, LANES), 1)
    row = lax.broadcasted_iota(jnp.int32, (VIEW, LANES), 0)
    return (lane & 32) != 0, (lane & 64) != 0, (row & 4) != 0


def turn():
    return lax.rem(lax.axis_index("gy"), 4)


def first_kernel(density_hbm, deriv_hbm, send_ref, density_ref, deriv_ref, sems):
    copies = [
        pltpu.make_async_copy(density_hbm, density_ref, sems.at[0]),
        pltpu.make_async_copy(deriv_hbm, deriv_ref, sems.at[1]),
    ]
    for copy in copies:
        copy.start()
    back = 4 - turn()
    copies[0].wait()
    lines = jnp.concatenate(
        [density_ref[4 * (place // 4) + lax.rem(place % 4 + back, 4)] for place in range(16)]
    )
    turned = lines.T
    copies[1].wait()
    slopes = mul((deriv_ref[0], deriv_ref[1]), halves(turned))
    rows = 2 * VIEW
    for field, values in enumerate((turned, slopes)):
        for plane in range(2):
            for part in range(4):
                send_ref[pl.ds(VIEW * field + 4 * plane + part, LANES, stride=rows), :] = values[
                    LANES * plane : LANES * (plane + 1), LANES * part : LANES * (part + 1)
                ]


def middle_kernel(
    got_ref, deriv_x_ref, deriv_y_ref, send_ref, dens_ref, grad_z_ref, grad_x_ref, grad_y_ref
):
    rows = 2 * VIEW
    odd, upper, below = masks()

    def receive(step, carry):
        for inner in range(GROUP):
            a = step * GROUP + inner
            for field, ref in enumerate((dens_ref, grad_z_ref)):
                for half in range(2):
                    parts = []
                    for quarter in range(4):
                        start = a * (8 * rows) + ((half * 4 + quarter) * rows + VIEW * field)
                        parts.append(got_ref[pl.ds(pl.multiple_of(start, VIEW), VIEW), :])
                    parts = [
                        pltpu.roll(part, LANES - 32 * t, 1) if t else part
                        for t, part in enumerate(mix(parts, odd, upper))
                    ]
                    for pair in range(2):
                        start = pl.multiple_of(a * 16 + pair * VIEW, VIEW)
                        planes = swap_rows(parts[2 * pair], parts[2 * pair + 1], below)
                        for plane in range(2):
                            ref[
                                plane, pl.ds(start, VIEW), LANES * half : LANES * (half + 1)
                            ] = planes[plane]
        return carry

    lax.fori_loop(0, 16 // GROUP, receive, 0)
    deriv_x = deriv_x_ref[0], deriv_x_ref[1]
    deriv_y = deriv_y_ref[0], deriv_y_ref[1]
    for plane in range(2):
        dens = halves(dens_ref[plane])
        grad_x_ref[plane] = mul(deriv_x, dens)
        grad_y_ref[plane] = mul(dens, deriv_y)

    def evaluate(step, total):
        plane, start = lax.div(step, 256 // BLOCK), lax.rem(step, 256 // BLOCK) * BLOCK
        block = plane, pl.ds(pl.multiple_of(start, BLOCK), BLOCK)
        n = dens_ref[block]
        gx, gy, gz = grad_x_ref[block], grad_y_ref[block], grad_z_ref[block]
        f, d_dens, twice = pbe(n, gx * gx + gy * gy + gz * gz)
        grad_x_ref[block] = twice * gx
        grad_y_ref[block] = twice * gy
        grad_z_ref[block] = twice * gz
        dens_ref[block] = d_dens
        return total + f

    total = lax.fori_loop(0, 512 // BLOCK, evaluate, jnp.zeros((BLOCK, 256), jnp.float32))
    for plane in range(2):
        dens_ref[plane] = (
            dens_ref[plane]
            - mul(deriv_x, halves(grad_x_ref[plane]))
            - mul(halves(grad_y_ref[plane]), deriv_y)
        )

    def give(step, carry):
        for inner in range(GROUP):
            a = step * GROUP + inner
            for field, ref in enumerate((dens_ref, grad_z_ref)):
                for half in range(2):
                    parts = []
                    for pair in range(2):
                        start = pl.multiple_of(a * 16 + pair * VIEW, VIEW)
                        planes = [
                            ref[plane, pl.ds(start, VIEW), LANES * half : LANES * (half + 1)]
                            for plane in range(2)
                        ]
                        parts.extend(swap_rows(*planes, below))
                    parts = [
                        pltpu.roll(part, 32 * t, 1) if t else part for t, part in enumerate(parts)
                    ]
                    for quarter, part in enumerate(mix(parts, odd, upper)):
                        start = (half * 4 + quarter) * (rows + 1) + VIEW * field
                        send_ref[pl.ds(a * (8 * rows + 8) + start, VIEW), :] = part
        return carry

    lax.fori_loop(0, 16 // GROUP, give, 0)
    summed = jnp.sum(total[:, :LANES] + total[:, LANES:], axis=0, keepdims=True)
    send_ref[pl.ds(rows, LANES, stride=rows + 1), :] = jnp.broadcast_to(summed, (LANES, LANES))


def last_kernel(cells, got_ref, deriv_ref, potential_ref, energy_ref):
    rows = 2 * VIEW + 1
    back = 4 - turn()

    def gather(field):
        return jnp.concatenate(
            [
                jnp.concatenate(
                    [
                        got_ref[pl.ds(VIEW * field + 4 * plane + part, LANES, stride=rows), :]
                        for part in range(4)
                    ],
                    axis=1,
                )
                for plane in range(2)
            ],
            axis=0,
        )

    turned = gather(0) - mul((deriv_ref[0], deriv_ref[1]), halves(gather(1)))
    lines = turned.T
    for place in range(16):
        potential_ref[4 * (place // 4) + lax.rem(place % 4 + back, 4)] = lines[
            32 * place : 32 * (place + 1)
        ]
    energy_ref[0, 0] = jnp.sum(got_ref[pl.ds(rows - 1, LANES, stride=rows), :]) / cells


def params(megabytes):
    return pltpu.CompilerParams(vmem_limit_bytes=megabytes << 20)


def in_vmem(count):
    return [pl.BlockSpec(memory_space=pltpu.VMEM)] * count


def far(values):
    return pltpu.with_memory_space_constraint(values, pltpu.HBM)


def exchange(values):
    return lax.all_to_all(values, AXES, split_axis=0, concat_axis=0, tiled=True)


def pair(matrix):
    high = matrix.astype(jnp.bfloat16)
    low = (matrix - high.astype(np.float64)).astype(jnp.bfloat16)
    return jnp.asarray(np.stack([high, low]))


def body(cells, density):
    count = density.shape[-1]
    deriv = deriv_matrix(count)
    row = np.arange(count)
    cell = 16 * (row // 16) + 4 * (row % 4) + (row // 4) % 4
    deriv_z = pair(deriv)
    deriv_y = pair(deriv.T)
    deriv_x = pair(deriv[cell[:, None], cell[None, :]])

    send = pl.pallas_call(
        first_kernel,
        out_shape=jax.ShapeDtypeStruct((2048, LANES), jnp.float32),
        in_specs=[pl.BlockSpec(memory_space=pltpu.HBM)] * 2,
        out_specs=pl.BlockSpec(memory_space=pltpu.VMEM),
        scratch_shapes=[
            pltpu.VMEM(density.shape, jnp.float32),
            pltpu.VMEM((2, count, count), jnp.bfloat16),
            pltpu.SemaphoreType.DMA((2,)),
        ],
        compiler_params=params(12),
    )(far(density), far(deriv_z))
    got = exchange(send.reshape(LANES, 16, LANES)).reshape(2048, LANES)
    send = pl.pallas_call(
        middle_kernel,
        out_shape=jax.ShapeDtypeStruct((17 * LANES, LANES), jnp.float32),
        in_specs=in_vmem(3),
        out_specs=pl.BlockSpec(memory_space=pltpu.VMEM),
        scratch_shapes=[pltpu.VMEM((2, count, count), jnp.float32)] * 4,
        compiler_params=params(16),
    )(got, deriv_x, deriv_y)
    got = exchange(send.reshape(LANES, 1, 17 * LANES)).reshape(17 * LANES, LANES)
    potential, energy = pl.pallas_call(
        functools.partial(last_kernel, float(cells)),
        out_shape=(
            jax.ShapeDtypeStruct(density.shape, jnp.float32),
            jax.ShapeDtypeStruct((1, 1), jnp.float32),
        ),
        in_specs=in_vmem(2),
        out_specs=(
            pl.BlockSpec(memory_space=pltpu.VMEM),
            pl.BlockSpec(memory_space=pltpu.SMEM),
        ),
        compiler_params=params(12),
    )(got, deriv_z)
    return potential, energy.reshape(())


def solution(mesh):
    return jax.shard_map(
        functools.partial(body, 256**3),
        mesh=mesh,
        in_specs=(P("gx", "gy", None),),
        out_specs=(P("gx", "gy", None), P()),
        check_vma=False,
    )
```

time: 72.7 us -> 63.2 us (0.87)
  Pallas kernels: 15.4 us -> 7.71 us
  blocking collectives: 56.4 us -> 54.6 us
    pallas_call x1, Pallas kernels: 9.49 us -> 4.36 us  [body(): pl.pallas_call(middle_kernel, out_shape=jax.ShapeDtypeStruct((17 * LANES,...]
    all_to_all x2, blocking collectives: 56.4 us -> 54.6 us  [exchange(): return lax.all_to_all(values, AXES, split_axis=0, concat_axis=0, tiled=True)]
    pallas_call x1, Pallas kernels: 2.89 us -> 1.36 us  [body(): pl.pallas_call(functools.partial(last_kernel, float(cells)), out_shape=(j...]
    pallas_call x1, Pallas kernels: 3.05 us -> 1.99 us  [body(): pl.pallas_call(first_kernel, out_shape=jax.ShapeDtypeStruct((2048, LANES)...]
where the time goes in v1:
time: 63.2 us; the launch traced here: 63 us
  blocking collectives  54.6 us (86%)
  Pallas kernels  7.71 us (12%)
  between operations  0.67 us (1%)
    all_to_all x2, blocking collectives, exchange(): return lax.all_to_all(values, AXES, split_axis=0, concat_axis=0, tiled=True)  54.6 us
    pallas_call x1, Pallas kernels, body(): pl.pallas_call(middle_kernel, out_shape=jax.ShapeDtypeStruct((17 * LANES,...  4.36 us
    pallas_call x1, Pallas kernels, body(): pl.pallas_call(first_kernel, out_shape=jax.ShapeDtypeStruct((2048, LANES)...  1.99 us
    pallas_call x1, Pallas kernels, body(): pl.pallas_call(functools.partial(last_kernel, float(cells)), out_shape=(j...  1.36 us

profile of v1, /device:TPU:1, one launch (start us, length us, event | category | flops | bytes accessed | tf_op | source)
XLA Modules:
  0.0 63.0 jit_solution(6385171890021745000)
XLA Ops:
  0.6 2.0 %shard_map.59 = f32[2048,128]{1,0:T(8,128)S(1)} custom-call(f32[16,32,256]{2,1,0:T(8,128)} %density_hbm.1, bf16[2,256,256]{2,1,0:T(8,128)(2,1)} %constant.6.clone.deriv_hbm.deriv_ref), custom_call_target="tpu_custom_call" | custom-call | tf_op jit(solution)/shard_map/pallas_call | solution.py:304
  2.6 0.0 copy-start.1
  2.6 0.0 copy-start.2
  2.6 30.7 %all_to_all.10 = f32[128,16,128]{2,1,0:T(8,128)S(1)} all-to-all(f32[128,16,128]{2,1,0:T(8,128)S(1)} %bitcast.7), channel_id=1, replica_groups=mesh['gx'=16,'gy'=8] {'gx','gy'}, dimensions={0} | all-to-all | bytes 2097152 | tf_op jit(solution)/shard_map/all_to_all | solution.py:286
  33.3 0.0 copy-done.1
  33.3 0.0 copy-done.2
  33.3 4.4 %shard_map.60 = f32[2176,128]{1,0:T(8,128)S(1)} custom-call(f32[2048,128]{1,0:T(8,128)S(1)} %bitcast.8, bf16[2,256,256]{2,1,0:T(8,128)(2,1)S(1)} %copy-done.1, bf16[2,256,256]{2,1,0:T(8,128)(2,1)S(1)} %copy-done.2), custom_call_target="tpu_custom_call" | custom-call | tf_op jit(solution)/shard_map/pallas_call | solution.py:317
  37.7 0.0 copy-start
  37.7 24.0 %all_to_all.11 = f32[128,1,2176]{2,1,0:T(1,128)S(1)} all-to-all(f32[128,1,2176]{2,1,0:T(1,128)S(1)} %bitcast.6), channel_id=1, replica_groups=mesh['gx'=16,'gy'=8] {'gx','gy'}, dimensions={0} | all-to-all | bytes 2228224 | tf_op jit(solution)/shard_map/all_to_all | solution.py:286
  61.7 0.0 copy-done
  61.7 1.4 %shard_map.61 = (f32[16,32,256]{2,1,0:T(8,128)}, f32[1,1]{1,0:T(1,128)}) custom-call(f32[2176,128]{1,0:T(8,128)S(1)} %bitcast.5, bf16[2,256,256]{2,1,0:T(8,128)(2,1)S(1)} %copy-done), custom_call_target="tpu_custom_call" | custom-call | tf_op jit(solution)/shard_map/pallas_call | solution.py:326
Async XLA Ops:
  2.6 30.7 %copy-start.1 = (bf16[2,256,256]{2,1,0:T(8,128)(2,1)S(1)}, bf16[2,256,256]{2,1,0:T(8,128)(2,1)}, u32[]{:S(2)}) copy-start(bf16[2,256,256]{2,1,0:T(8,128)(2,1)} %constant.8.clone.deriv_x_ref) | copy-start | bytes 786436
  2.6 30.7 %copy-start.2 = (bf16[2,256,256]{2,1,0:T(8,128)(2,1)S(1)}, bf16[2,256,256]{2,1,0:T(8,128)(2,1)}, u32[]{:S(2)}) copy-start(bf16[2,256,256]{2,1,0:T(8,128)(2,1)} %constant.7.clone.deriv_y_ref) | copy-start | bytes 786436
  37.7 24.0 %copy-start = (bf16[2,256,256]{2,1,0:T(8,128)(2,1)S(1)}, bf16[2,256,256]{2,1,0:T(8,128)(2,1)}, u32[]{:S(2)}) copy-start(bf16[2,256,256]{2,1,0:T(8,128)(2,1)} %constant.6.clone.deriv_hbm.deriv_ref) | copy-start | bytes 786436

commit v2 on v1

--- a/solution.py
+++ b/solution.py
@@ -12,7 +12,6 @@
 AXES = ("gx", "gy")
 LANES = 128
 VIEW = 8
-GROUP = 4
 BLOCK = 32
 
 pbe_kappa = 0.804
@@ -31,6 +30,7 @@
 s_scale = 1.0 / (4.0 * fermi_scale**2)
 t_scale = math.pi / (16.0 * fermi_scale)
 rs_scale = (3.0 / (4.0 * math.pi)) ** (1.0 / 3.0)
+ex_scale = -exch_scale / rs_scale**2
 root_slope = -1.0 / (6.0 * math.log(2.0))
 root_shift = 0.5 * math.log2(rs_scale)
 damping_scale = pbe_mu / pbe_kappa * s_scale / rs_scale**8
@@ -70,7 +70,7 @@
     scaled = g * rs4
     damping = 1.0 + damping_scale * (scaled * rs4)
     tau = tau_scale * (scaled * (rs2 * rs))
-    ex = (-exch_scale / rs_scale**2) * (n * rs2)
+    part = n * rs2
     series = root * (pw[0] + root * (pw[1] + root * (pw[2] + root * pw[3])))
     third = root * (
         pw[0] / 6 + root * (pw[1] / 3 + root * (pw[2] / 2 + root * (pw[3] / 1.5)))
@@ -96,17 +96,17 @@
     both = 1.0 / (base * top)
     rest = ec + pbe_gamma * jnp.log(top * (top * both))
     damp2 = damp * damp
-    energy = ex * ((1.0 + pbe_kappa) - pbe_kappa * damp) + rest
+    energy = part * ((1.0 + pbe_kappa) * ex_scale - (pbe_kappa * ex_scale) * damp) + rest
     weight = (near + tau) * (m2 * m)
     twice = rs4 * (slope_scale * damp2 + (weight_scale * weight) * both)
     n_dh = (tau * both) * (
         (-7.0 / 3.0 * pbe_gamma) * weight - tau2 * ((near + m) * (grown * n_dec))
     )
     d_dens = (
-        ex
+        part
         * (
-            (4.0 / 3.0) * (1.0 + pbe_kappa)
-            + damp * ((-4.0 * pbe_kappa) + (8.0 / 3.0 * pbe_kappa) * damp)
+            (4.0 / 3.0) * (1.0 + pbe_kappa) * ex_scale
+            + damp * ((-4.0 * pbe_kappa * ex_scale) + (8.0 / 3.0 * pbe_kappa * ex_scale) * damp)
         )
         + (rest + n_dec)
         + n_dh
@@ -136,7 +136,7 @@
     return lax.rem(lax.axis_index("gy"), 4)
 
 
-def first_kernel(density_hbm, deriv_hbm, send_ref, density_ref, deriv_ref, sems):
+def first_kernel(density_hbm, deriv_hbm, send_ref, density_ref, deriv_ref, wide_ref, sems):
     copies = [
         pltpu.make_async_copy(density_hbm, density_ref, sems.at[0]),
         pltpu.make_async_copy(deriv_hbm, deriv_ref, sems.at[1]),
@@ -155,9 +155,13 @@
     for field, values in enumerate((turned, slopes)):
         for plane in range(2):
             for part in range(4):
-                send_ref[pl.ds(VIEW * field + 4 * plane + part, LANES, stride=rows), :] = values[
+                row = VIEW * field + 4 * plane + part
+                wide_ref[pl.ds(row, LANES, stride=rows + 1), :] = values[
                     LANES * plane : LANES * (plane + 1), LANES * part : LANES * (part + 1)
                 ]
+    for other in range(LANES):
+        start = (rows + 1) * other
+        send_ref[rows * other : rows * (other + 1), :] = wide_ref[start : start + rows, :]
 
 
 def middle_kernel(
@@ -166,78 +170,78 @@
     rows = 2 * VIEW
     odd, upper, below = masks()
 
-    def receive(step, carry):
-        for inner in range(GROUP):
-            a = step * GROUP + inner
-            for field, ref in enumerate((dens_ref, grad_z_ref)):
-                for half in range(2):
-                    parts = []
-                    for quarter in range(4):
-                        start = a * (8 * rows) + ((half * 4 + quarter) * rows + VIEW * field)
-                        parts.append(got_ref[pl.ds(pl.multiple_of(start, VIEW), VIEW), :])
-                    parts = [
-                        pltpu.roll(part, LANES - 32 * t, 1) if t else part
-                        for t, part in enumerate(mix(parts, odd, upper))
-                    ]
-                    for pair in range(2):
-                        start = pl.multiple_of(a * 16 + pair * VIEW, VIEW)
-                        planes = swap_rows(parts[2 * pair], parts[2 * pair + 1], below)
-                        for plane in range(2):
-                            ref[
-                                plane, pl.ds(start, VIEW), LANES * half : LANES * (half + 1)
-                            ] = planes[plane]
-        return carry
-
-    lax.fori_loop(0, 16 // GROUP, receive, 0)
-    deriv_x = deriv_x_ref[0], deriv_x_ref[1]
-    deriv_y = deriv_y_ref[0], deriv_y_ref[1]
-    for plane in range(2):
+    def receive(a, field, ref):
+        for half in range(2):
+            parts = []
+            for quarter in range(4):
+                start = a * (8 * rows) + ((half * 4 + quarter) * rows + VIEW * field)
+                parts.append(got_ref[start : start + VIEW, :])
+            parts = [
+                pltpu.roll(part, LANES - 32 * t, 1) if t else part
+                for t, part in enumerate(mix(parts, odd, upper))
+            ]
+            for pair in range(2):
+                planes = swap_rows(parts[2 * pair], parts[2 * pair + 1], below)
+                for plane in range(2):
+                    start = a * 16 + pair * VIEW
+                    ref[
+                        plane, start : start + VIEW, LANES * half : LANES * (half + 1)
+                    ] = planes[plane]
+
+    def give(a, field, ref):
+        for half in range(2):
+            parts = []
+            for pair in range(2):
+                start = a * 16 + pair * VIEW
+                planes = [
+                    ref[plane, start : start + VIEW, LANES * half : LANES * (half + 1)]
+                    for plane in range(2)
+                ]
+                parts.extend(swap_rows(*planes, below))
+            parts = [pltpu.roll(part, 32 * t, 1) if t else part for t, part in enumerate(parts)]
+            for quarter, part in enumerate(mix(parts, odd, upper)):
+                start = ((a * 2 + half) * 4 + quarter) * (rows + 1) + VIEW * field
+                send_ref[start : start + VIEW, :] = part
+
+    def slopes(plane):
         dens = halves(dens_ref[plane])
-        grad_x_ref[plane] = mul(deriv_x, dens)
-        grad_y_ref[plane] = mul(dens, deriv_y)
-
-    def evaluate(step, total):
-        plane, start = lax.div(step, 256 // BLOCK), lax.rem(step, 256 // BLOCK) * BLOCK
-        block = plane, pl.ds(pl.multiple_of(start, BLOCK), BLOCK)
-        n = dens_ref[block]
-        gx, gy, gz = grad_x_ref[block], grad_y_ref[block], grad_z_ref[block]
-        f, d_dens, twice = pbe(n, gx * gx + gy * gy + gz * gz)
-        grad_x_ref[block] = twice * gx
-        grad_y_ref[block] = twice * gy
-        grad_z_ref[block] = twice * gz
-        dens_ref[block] = d_dens
-        return total + f
-
-    total = lax.fori_loop(0, 512 // BLOCK, evaluate, jnp.zeros((BLOCK, 256), jnp.float32))
-    for plane in range(2):
+        grad_x_ref[plane] = mul((deriv_x_ref[0], deriv_x_ref[1]), dens)
+        grad_y_ref[plane] = mul(dens, (deriv_y_ref[0], deriv_y_ref[1]))
+
+    def subtract(plane):
         dens_ref[plane] = (
             dens_ref[plane]
-            - mul(deriv_x, halves(grad_x_ref[plane]))
-            - mul(halves(grad_y_ref[plane]), deriv_y)
+            - mul((deriv_x_ref[0], deriv_x_ref[1]), halves(grad_x_ref[plane]))
+            - mul(halves(grad_y_ref[plane]), (deriv_y_ref[0], deriv_y_ref[1]))
         )
 
-    def give(step, carry):
-        for inner in range(GROUP):
-            a = step * GROUP + inner
-            for field, ref in enumerate((dens_ref, grad_z_ref)):
-                for half in range(2):
-                    parts = []
-                    for pair in range(2):
-                        start = pl.multiple_of(a * 16 + pair * VIEW, VIEW)
-                        planes = [
-                            ref[plane, pl.ds(start, VIEW), LANES * half : LANES * (half + 1)]
-                            for plane in range(2)
-                        ]
-                        parts.extend(swap_rows(*planes, below))
-                    parts = [
-                        pltpu.roll(part, 32 * t, 1) if t else part for t, part in enumerate(parts)
-                    ]
-                    for quarter, part in enumerate(mix(parts, odd, upper)):
-                        start = (half * 4 + quarter) * (rows + 1) + VIEW * field
-                        send_ref[pl.ds(a * (8 * rows + 8) + start, VIEW), :] = part
-        return carry
-
-    lax.fori_loop(0, 16 // GROUP, give, 0)
+    def evaluate(plane, total):
+        for start in range(0, 256, BLOCK):
+            block = plane, slice(start, start + BLOCK)
+            n = dens_ref[block]
+            gx, gy, gz = grad_x_ref[block], grad_y_ref[block], grad_z_ref[block]
+            f, d_dens, twice = pbe(n, gx * gx + gy * gy + gz * gz)
+            grad_x_ref[block] = twice * gx
+            grad_y_ref[block] = twice * gy
+            grad_z_ref[block] = twice * gz
+            dens_ref[block] = d_dens
+            total = total + f
+        return total
+
+    for a in range(16):
+        receive(a, 0, dens_ref)
+    slopes(0)
+    for a in range(16):
+        receive(a, 1, grad_z_ref)
+    total = evaluate(0, jnp.zeros((BLOCK, 256), jnp.float32))
+    slopes(1)
+    subtract(0)
+    total = evaluate(1, total)
+    subtract(1)
+    for a in range(16):
+        give(a, 1, grad_z_ref)
+    for a in range(16):
+        give(a, 0, dens_ref)
     summed = jnp.sum(total[:, :LANES] + total[:, LANES:], axis=0, keepdims=True)
     send_ref[pl.ds(rows, LANES, stride=rows + 1), :] = jnp.broadcast_to(summed, (LANES, LANES))
 
@@ -309,6 +313,7 @@
         scratch_shapes=[
             pltpu.VMEM(density.shape, jnp.float32),
             pltpu.VMEM((2, count, count), jnp.bfloat16),
+            pltpu.VMEM((17 * LANES, LANES), jnp.float32),
             pltpu.SemaphoreType.DMA((2,)),
         ],
         compiler_params=params(12),

time: 63.2 us -> 61.3 us (0.970)
  Pallas kernels: 7.71 us -> 5.79 us
    pallas_call x1, Pallas kernels: 4.36 us -> 2.69 us  [body(): pl.pallas_call(middle_kernel, out_shape=jax.ShapeDtypeStruct((17 * LANES,...]
where the time goes in v2:
time: 61.3 us; the launch traced here: 61.1 us
  blocking collectives  54.6 us (89%)
  Pallas kernels  5.79 us (9%)
  between operations  0.66 us (1%)
    all_to_all x2, blocking collectives, exchange(): return lax.all_to_all(values, AXES, split_axis=0, concat_axis=0, tiled=True)  54.6 us
    pallas_call x1, Pallas kernels, body(): pl.pallas_call(middle_kernel, out_shape=jax.ShapeDtypeStruct((17 * LANES,...  2.69 us
    pallas_call x1, Pallas kernels, body(): pl.pallas_call(first_kernel, out_shape=jax.ShapeDtypeStruct((2048, LANES)...  1.74 us
    pallas_call x1, Pallas kernels, body(): pl.pallas_call(functools.partial(last_kernel, float(cells)), out_shape=(j...  1.36 us

profile of v2, /device:TPU:1, one launch (start us, length us, event | category | flops | bytes accessed | tf_op | source)
XLA Modules:
  0.0 61.1 jit_solution(11163598833392544072)
XLA Ops:
  0.6 1.7 %shard_map.59 = f32[2048,128]{1,0:T(8,128)S(1)} custom-call(f32[16,32,256]{2,1,0:T(8,128)} %density_hbm.1, bf16[2,256,256]{2,1,0:T(8,128)(2,1)} %constant.6.clone.deriv_hbm.deriv_ref), custom_call_target="tpu_custom_call" | custom-call | tf_op jit(solution)/shard_map/pallas_call | solution.py:308
  2.4 0.0 copy-start.1
  2.4 0.0 copy-start.2
  2.4 30.7 %all_to_all.10 = f32[128,16,128]{2,1,0:T(8,128)S(1)} all-to-all(f32[128,16,128]{2,1,0:T(8,128)S(1)} %bitcast.7), channel_id=1, replica_groups=mesh['gx'=16,'gy'=8] {'gx','gy'}, dimensions={0} | all-to-all | bytes 2097152 | tf_op jit(solution)/shard_map/all_to_all | solution.py:290
  33.1 0.0 copy-done.1
  33.1 0.0 copy-done.2
  33.1 2.7 %shard_map.60 = f32[2176,128]{1,0:T(8,128)S(1)} custom-call(f32[2048,128]{1,0:T(8,128)S(1)} %bitcast.8, bf16[2,256,256]{2,1,0:T(8,128)(2,1)S(1)} %copy-done.1, bf16[2,256,256]{2,1,0:T(8,128)(2,1)S(1)} %copy-done.2), custom_call_target="tpu_custom_call" | custom-call | tf_op jit(solution)/shard_map/pallas_call | solution.py:322
  35.8 0.0 copy-start
  35.8 24.0 %all_to_all.11 = f32[128,1,2176]{2,1,0:T(1,128)S(1)} all-to-all(f32[128,1,2176]{2,1,0:T(1,128)S(1)} %bitcast.6), channel_id=1, replica_groups=mesh['gx'=16,'gy'=8] {'gx','gy'}, dimensions={0} | all-to-all | bytes 2228224 | tf_op jit(solution)/shard_map/all_to_all | solution.py:290
  59.8 0.0 copy-done
  59.8 1.4 %shard_map.61 = (f32[16,32,256]{2,1,0:T(8,128)}, f32[1,1]{1,0:T(1,128)}) custom-call(f32[2176,128]{1,0:T(8,128)S(1)} %bitcast.5, bf16[2,256,256]{2,1,0:T(8,128)(2,1)S(1)} %copy-done), custom_call_target="tpu_custom_call" | custom-call | tf_op jit(solution)/shard_map/pallas_call | solution.py:331
Async XLA Ops:
  2.4 30.7 %copy-start.1 = (bf16[2,256,256]{2,1,0:T(8,128)(2,1)S(1)}, bf16[2,256,256]{2,1,0:T(8,128)(2,1)}, u32[]{:S(2)}) copy-start(bf16[2,256,256]{2,1,0:T(8,128)(2,1)} %constant.8.clone.deriv_x_ref) | copy-start | bytes 786436
  2.4 30.7 %copy-start.2 = (bf16[2,256,256]{2,1,0:T(8,128)(2,1)S(1)}, bf16[2,256,256]{2,1,0:T(8,128)(2,1)}, u32[]{:S(2)}) copy-start(bf16[2,256,256]{2,1,0:T(8,128)(2,1)} %constant.7.clone.deriv_y_ref) | copy-start | bytes 786436
  35.8 24.0 %copy-start = (bf16[2,256,256]{2,1,0:T(8,128)(2,1)S(1)}, bf16[2,256,256]{2,1,0:T(8,128)(2,1)}, u32[]{:S(2)}) copy-start(bf16[2,256,256]{2,1,0:T(8,128)(2,1)} %constant.6.clone.deriv_hbm.deriv_ref) | copy-start | bytes 786436

commit v3 on v2

--- a/solution.py
+++ b/solution.py
@@ -55,9 +55,11 @@
     return high, (values - high.astype(jnp.float32)).astype(jnp.bfloat16)
 
 
-def mul(left, right):
+def mul(left, right, axis=0):
     def dot(first, second):
-        return jnp.dot(first, second, preferred_element_type=jnp.float32)
+        return lax.dot_general(
+            first, second, (((1,), (axis,)), ((), ())), preferred_element_type=jnp.float32
+        )
 
     return dot(left[0], right[0]) + dot(left[1], right[0]) + dot(left[0], right[1])
 
@@ -75,12 +77,10 @@
     third = root * (
         pw[0] / 6 + root * (pw[1] / 3 + root * (pw[2] / 2 + root * (pw[3] / 1.5)))
     )
-    outer = 1.0 + series
-    product = series * outer
-    inverse = 1.0 / (product * damping)
-    damp = product * inverse
-    fraction = damping * inverse
-    logarithm = jnp.log(1.0 + outer * fraction)
+    damp = 1.0 / damping
+    flipped = 1.0 / series
+    fraction = flipped * (1.0 / (1.0 + series))
+    logarithm = jnp.log(1.0 + flipped)
     curved = (-2.0 * pw_coef * pw_alpha) * rs
     front = curved - 2.0 * pw_coef
     ec = front * logarithm
@@ -93,8 +93,9 @@
     near = m + tau
     base = m2 + cross + tau2
     top = base + cross * near
-    both = 1.0 / (base * top)
-    rest = ec + pbe_gamma * jnp.log(top * (top * both))
+    lower = 1.0 / base
+    both = lower * (1.0 / top)
+    rest = ec + pbe_gamma * jnp.log(top * lower)
     damp2 = damp * damp
     energy = part * ((1.0 + pbe_kappa) * ex_scale - (pbe_kappa * ex_scale) * damp) + rest
     weight = (near + tau) * (m2 * m)
@@ -144,13 +145,13 @@
     for copy in copies:
         copy.start()
     back = 4 - turn()
-    copies[0].wait()
+    for copy in copies:
+        copy.wait()
     lines = jnp.concatenate(
         [density_ref[4 * (place // 4) + lax.rem(place % 4 + back, 4)] for place in range(16)]
     )
     turned = lines.T
-    copies[1].wait()
-    slopes = mul((deriv_ref[0], deriv_ref[1]), halves(turned))
+    slopes = mul((deriv_ref[0], deriv_ref[1]), halves(lines), 1)
     rows = 2 * VIEW
     for field, values in enumerate((turned, slopes)):
         for plane in range(2):

time: 61.3 us -> 61.1 us (level)
  no operation moved by 1% of the time
where the time goes in v3:
time: 61.1 us; the launch traced here: 60.9 us
  blocking collectives  54.7 us (90%)
  Pallas kernels  5.57 us (9%)
  between operations  0.67 us (1%)
    all_to_all x2, blocking collectives, exchange(): return lax.all_to_all(values, AXES, split_axis=0, concat_axis=0, tiled=True)  54.7 us
    pallas_call x1, Pallas kernels, body(): pl.pallas_call(middle_kernel, out_shape=jax.ShapeDtypeStruct((17 * LANES,...  2.62 us
    pallas_call x1, Pallas kernels, body(): pl.pallas_call(first_kernel, out_shape=jax.ShapeDtypeStruct((2048, LANES)...  1.59 us
    pallas_call x1, Pallas kernels, body(): pl.pallas_call(functools.partial(last_kernel, float(cells)), out_shape=(j...  1.36 us

profile of v3, /device:TPU:1, one launch (start us, length us, event | category | flops | bytes accessed | tf_op | source)
XLA Modules:
  0.0 60.9 jit_solution(11808422718603608668)
XLA Ops:
  0.6 1.6 %shard_map.59 = f32[2048,128]{1,0:T(8,128)S(1)} custom-call(f32[16,32,256]{2,1,0:T(8,128)} %density_hbm.1, bf16[2,256,256]{2,1,0:T(8,128)(2,1)} %constant.6.clone.deriv_hbm.deriv_ref), custom_call_target="tpu_custom_call" | custom-call | tf_op jit(solution)/shard_map/pallas_call | solution.py:309
  2.2 0.0 copy-start.1
  2.2 0.0 copy-start.2
  2.3 30.7 %all_to_all.10 = f32[128,16,128]{2,1,0:T(8,128)S(1)} all-to-all(f32[128,16,128]{2,1,0:T(8,128)S(1)} %bitcast.7), channel_id=1, replica_groups=mesh['gx'=16,'gy'=8] {'gx','gy'}, dimensions={0} | all-to-all | bytes 2097152 | tf_op jit(solution)/shard_map/all_to_all | solution.py:291
  33.0 0.0 copy-done.1
  33.0 0.0 copy-done.2
  33.0 2.6 %shard_map.60 = f32[2176,128]{1,0:T(8,128)S(1)} custom-call(f32[2048,128]{1,0:T(8,128)S(1)} %bitcast.8, bf16[2,256,256]{2,1,0:T(8,128)(2,1)S(1)} %copy-done.1, bf16[2,256,256]{2,1,0:T(8,128)(2,1)S(1)} %copy-done.2), custom_call_target="tpu_custom_call" | custom-call | tf_op jit(solution)/shard_map/pallas_call | solution.py:323
  35.6 0.0 copy-start
  35.6 23.9 %all_to_all.11 = f32[128,1,2176]{2,1,0:T(1,128)S(1)} all-to-all(f32[128,1,2176]{2,1,0:T(1,128)S(1)} %bitcast.6), channel_id=1, replica_groups=mesh['gx'=16,'gy'=8] {'gx','gy'}, dimensions={0} | all-to-all | bytes 2228224 | tf_op jit(solution)/shard_map/all_to_all | solution.py:291
  59.5 0.0 copy-done
  59.6 1.4 %shard_map.61 = (f32[16,32,256]{2,1,0:T(8,128)}, f32[1,1]{1,0:T(1,128)}) custom-call(f32[2176,128]{1,0:T(8,128)S(1)} %bitcast.5, bf16[2,256,256]{2,1,0:T(8,128)(2,1)S(1)} %copy-done), custom_call_target="tpu_custom_call" | custom-call | tf_op jit(solution)/shard_map/pallas_call | solution.py:332
Async XLA Ops:
  2.2 30.7 %copy-start.1 = (bf16[2,256,256]{2,1,0:T(8,128)(2,1)S(1)}, bf16[2,256,256]{2,1,0:T(8,128)(2,1)}, u32[]{:S(2)}) copy-start(bf16[2,256,256]{2,1,0:T(8,128)(2,1)} %constant.8.clone.deriv_x_ref) | copy-start | bytes 786436
  2.2 30.7 %copy-start.2 = (bf16[2,256,256]{2,1,0:T(8,128)(2,1)S(1)}, bf16[2,256,256]{2,1,0:T(8,128)(2,1)}, u32[]{:S(2)}) copy-start(bf16[2,256,256]{2,1,0:T(8,128)(2,1)} %constant.7.clone.deriv_y_ref) | copy-start | bytes 786436
  35.6 24.0 %copy-start = (bf16[2,256,256]{2,1,0:T(8,128)(2,1)S(1)}, bf16[2,256,256]{2,1,0:T(8,128)(2,1)}, u32[]{:S(2)}) copy-start(bf16[2,256,256]{2,1,0:T(8,128)(2,1)} %constant.6.clone.deriv_hbm.deriv_ref) | copy-start | bytes 786436

commit v4 on v3

--- a/solution.py
+++ b/solution.py
@@ -7,9 +7,12 @@
 from jax import lax
 from jax.experimental import pallas as pl
 from jax.experimental.pallas import tpu as pltpu
+from jax.sharding import Mesh
 from jax.sharding import PartitionSpec as P
 
-AXES = ("gx", "gy")
+GX = ("z1", "z0", "yh", "core")
+GY = ("yl", "x1", "x0")
+ORDER = ("core", "yh", "yl", "x1", "x0", "z1", "z0")
 LANES = 128
 VIEW = 8
 BLOCK = 32
@@ -120,11 +123,10 @@
     return [jnp.where(upper, pairs[(t + 2) % 4], pairs[t]) for t in range(4)]
 
 
-def swap_rows(first, second, below):
-    return (
-        jnp.where(below, pltpu.roll(second, 4, 0), first),
-        jnp.where(below, second, pltpu.roll(first, 4, 0)),
-    )
+def place(a, b):
+    at = {axis: a >> (3 - i) & 1 for i, axis in enumerate(GX)}
+    at |= {axis: b >> (2 - i) & 1 for i, axis in enumerate(GY)}
+    return functools.reduce(lambda index, axis: 2 * index + at[axis], ORDER, 0)
 
 
 def masks():
@@ -134,7 +136,7 @@
 
 
 def turn():
-    return lax.rem(lax.axis_index("gy"), 4)
+    return 2 * lax.axis_index("x1") + lax.axis_index("x0")
 
 
 def first_kernel(density_hbm, deriv_hbm, send_ref, density_ref, deriv_ref, wide_ref, sems):
@@ -171,38 +173,41 @@
     rows = 2 * VIEW
     odd, upper, below = masks()
 
-    def receive(a, field, ref):
+    def receive(pair, field, ref):
         for half in range(2):
-            parts = []
-            for quarter in range(4):
-                start = a * (8 * rows) + ((half * 4 + quarter) * rows + VIEW * field)
-                parts.append(got_ref[start : start + VIEW, :])
-            parts = [
-                pltpu.roll(part, LANES - 32 * t, 1) if t else part
-                for t, part in enumerate(mix(parts, odd, upper))
-            ]
-            for pair in range(2):
-                planes = swap_rows(parts[2 * pair], parts[2 * pair + 1], below)
-                for plane in range(2):
-                    start = a * 16 + pair * VIEW
-                    ref[
-                        plane, start : start + VIEW, LANES * half : LANES * (half + 1)
-                    ] = planes[plane]
-
-    def give(a, field, ref):
+            for plane in range(2):
+                parts = []
+                for quarter in range(4):
+                    block = 4 * half + quarter
+                    shift = VIEW * field + 4 * plane
+                    start = place(2 * pair, block) * rows + shift
+                    later = place(2 * pair + 1, block) * rows + shift - 4
+                    parts.append(
+                        jnp.where(
+                            below, got_ref[later : later + VIEW, :], got_ref[start : start + VIEW, :]
+                        )
+                    )
+                for t, part in enumerate(mix(parts, odd, upper)):
+                    start = (pair * 4 + t) * VIEW
+                    ref[plane, start : start + VIEW, LANES * half : LANES * (half + 1)] = (
+                        pltpu.roll(part, LANES - 32 * t, 1) if t else part
+                    )
+
+    def give(pair, field, ref):
         for half in range(2):
-            parts = []
-            for pair in range(2):
-                start = a * 16 + pair * VIEW
-                planes = [
-                    ref[plane, start : start + VIEW, LANES * half : LANES * (half + 1)]
-                    for plane in range(2)
-                ]
-                parts.extend(swap_rows(*planes, below))
-            parts = [pltpu.roll(part, 32 * t, 1) if t else part for t, part in enumerate(parts)]
-            for quarter, part in enumerate(mix(parts, odd, upper)):
-                start = ((a * 2 + half) * 4 + quarter) * (rows + 1) + VIEW * field
-                send_ref[start : start + VIEW, :] = part
+            for plane in range(2):
+                parts = []
+                for t in range(4):
+                    start = (pair * 4 + t) * VIEW
+                    part = ref[plane, start : start + VIEW, LANES * half : LANES * (half + 1)]
+                    parts.append(pltpu.roll(part, 32 * t, 1) if t else part)
+                for quarter, part in enumerate(mix(parts, odd, upper)):
+                    block = 4 * half + quarter
+                    shift = VIEW * field + 4 * plane
+                    start = place(2 * pair, block) * (rows + 1) + shift
+                    later = place(2 * pair + 1, block) * (rows + 1) + shift
+                    send_ref[start : start + 4, :] = part[:4]
+                    send_ref[later : later + 4, :] = part[4:]
 
     def slopes(plane):
         dens = halves(dens_ref[plane])
@@ -229,20 +234,20 @@
             total = total + f
         return total
 
-    for a in range(16):
-        receive(a, 0, dens_ref)
+    for pair in range(8):
+        receive(pair, 0, dens_ref)
     slopes(0)
-    for a in range(16):
-        receive(a, 1, grad_z_ref)
+    for pair in range(8):
+        receive(pair, 1, grad_z_ref)
     total = evaluate(0, jnp.zeros((BLOCK, 256), jnp.float32))
     slopes(1)
     subtract(0)
     total = evaluate(1, total)
     subtract(1)
-    for a in range(16):
-        give(a, 1, grad_z_ref)
-    for a in range(16):
-        give(a, 0, dens_ref)
+    for pair in range(8):
+        give(pair, 1, grad_z_ref)
+    for pair in range(8):
+        give(pair, 0, dens_ref)
     summed = jnp.sum(total[:, :LANES] + total[:, LANES:], axis=0, keepdims=True)
     send_ref[pl.ds(rows, LANES, stride=rows + 1), :] = jnp.broadcast_to(summed, (LANES, LANES))
 
@@ -288,7 +293,7 @@
 
 
 def exchange(values):
-    return lax.all_to_all(values, AXES, split_axis=0, concat_axis=0, tiled=True)
+    return lax.all_to_all(values, ORDER, split_axis=0, concat_axis=0, tiled=True)
 
 
 def pair(matrix):
@@ -301,7 +306,7 @@
     count = density.shape[-1]
     deriv = deriv_matrix(count)
     row = np.arange(count)
-    cell = 16 * (row // 16) + 4 * (row % 4) + (row // 4) % 4
+    cell = 16 * (2 * (row // 32) + (row // 4) % 2) + 4 * (row % 4) + (row // 8) % 4
     deriv_z = pair(deriv)
     deriv_y = pair(deriv.T)
     deriv_x = pair(deriv[cell[:, None], cell[None, :]])
@@ -346,10 +351,11 @@
 
 
 def solution(mesh):
+    split = Mesh(mesh.devices.reshape((2,) * 7), GX + GY)
     return jax.shard_map(
         functools.partial(body, 256**3),
-        mesh=mesh,
-        in_specs=(P("gx", "gy", None),),
-        out_specs=(P("gx", "gy", None), P()),
+        mesh=split,
+        in_specs=(P(GX, GY, None),),
+        out_specs=(P(GX, GY, None), P()),
         check_vma=False,
     )

time: 61.1 us -> 59.1 us (0.967)
  blocking collectives: 54.7 us -> 52.7 us
    all_to_all x2, blocking collectives: 54.7 us -> 52.7 us  [exchange(): lax.all_to_all(values, ORDER, split_axis=0, concat_axis=0, tiled=True)]
where the time goes in v4:
time: 59.1 us; the launch traced here: 59 us
  blocking collectives  52.7 us (89%)
  Pallas kernels  5.56 us (9%)
  between operations  0.66 us (1%)
    all_to_all x2, blocking collectives, exchange(): lax.all_to_all(values, ORDER, split_axis=0, concat_axis=0, tiled=True)  52.7 us
    pallas_call x1, Pallas kernels, body(): pl.pallas_call(middle_kernel, out_shape=jax.ShapeDtypeStruct((17 * LANES,...  2.61 us
    pallas_call x1, Pallas kernels, body(): pl.pallas_call(first_kernel, out_shape=jax.ShapeDtypeStruct((2048, LANES)...  1.59 us
    pallas_call x1, Pallas kernels, body(): pl.pallas_call(functools.partial(last_kernel, float(cells)), out_shape=(j...  1.36 us

profile of v4, /device:TPU:1, one launch (start us, length us, event | category | flops | bytes accessed | tf_op | source)
XLA Modules:
  0.0 59.0 jit_solution(4929233923963047187)
XLA Ops:
  0.6 1.6 %shard_map.59 = f32[2048,128]{1,0:T(8,128)S(1)} custom-call(f32[16,32,256]{2,1,0:T(8,128)} %density_hbm.1, bf16[2,256,256]{2,1,0:T(8,128)(2,1)} %constant.6.clone.deriv_hbm.deriv_ref), custom_call_target="tpu_custom_call" | custom-call | tf_op jit(solution)/shard_map/pallas_call | solution.py:314
  2.2 0.0 copy-start.1
  2.2 0.0 copy-start.2
  2.3 29.0 %all_to_all.10 = f32[128,16,128]{2,1,0:T(8,128)S(1)} all-to-all(f32[128,16,128]{2,1,0:T(8,128)S(1)} %bitcast.7), channel_id=1, replica_groups=mesh['z1'=2,'z0'=2,'yh'=2,'core'=2,'yl'=2,'x1'=2,'x0'=2] {'core','yh','y..., dimensions={0} | all-to-all | bytes 2097152 | tf_op jit(solution)/shard_map/all_to_all | solution.py:296
  31.3 0.0 copy-done.1
  31.3 0.0 copy-done.2
  31.3 2.6 %shard_map.60 = f32[2176,128]{1,0:T(8,128)S(1)} custom-call(f32[2048,128]{1,0:T(8,128)S(1)} %bitcast.8, bf16[2,256,256]{2,1,0:T(8,128)(2,1)S(1)} %copy-done.1, bf16[2,256,256]{2,1,0:T(8,128)(2,1)S(1)} %copy-done.2), custom_call_target="tpu_custom_call" | custom-call | tf_op jit(solution)/shard_map/pallas_call | solution.py:328
  33.9 0.0 copy-start
  33.9 23.7 %all_to_all.11 = f32[128,1,2176]{2,1,0:T(1,128)S(1)} all-to-all(f32[128,1,2176]{2,1,0:T(1,128)S(1)} %bitcast.6), channel_id=1, replica_groups=mesh['z1'=2,'z0'=2,'yh'=2,'core'=2,'yl'=2,'x1'=2,'x0'=2] {'core','yh','y..., dimensions={0} | all-to-all | bytes 2228224 | tf_op jit(solution)/shard_map/all_to_all | solution.py:296
  57.6 0.0 copy-done
  57.6 1.4 %shard_map.61 = (f32[16,32,256]{2,1,0:T(8,128)}, f32[1,1]{1,0:T(1,128)}) custom-call(f32[2176,128]{1,0:T(8,128)S(1)} %bitcast.5, bf16[2,256,256]{2,1,0:T(8,128)(2,1)S(1)} %copy-done), custom_call_target="tpu_custom_call" | custom-call | tf_op jit(solution)/shard_map/pallas_call | solution.py:337
Async XLA Ops:
  2.2 29.0 %copy-start.1 = (bf16[2,256,256]{2,1,0:T(8,128)(2,1)S(1)}, bf16[2,256,256]{2,1,0:T(8,128)(2,1)}, u32[]{:S(2)}) copy-start(bf16[2,256,256]{2,1,0:T(8,128)(2,1)} %constant.8.clone.deriv_x_ref) | copy-start | bytes 786436
  2.2 29.0 %copy-start.2 = (bf16[2,256,256]{2,1,0:T(8,128)(2,1)S(1)}, bf16[2,256,256]{2,1,0:T(8,128)(2,1)}, u32[]{:S(2)}) copy-start(bf16[2,256,256]{2,1,0:T(8,128)(2,1)} %constant.7.clone.deriv_y_ref) | copy-start | bytes 786436
  33.9 23.7 %copy-start = (bf16[2,256,256]{2,1,0:T(8,128)(2,1)S(1)}, bf16[2,256,256]{2,1,0:T(8,128)(2,1)}, u32[]{:S(2)}) copy-start(bf16[2,256,256]{2,1,0:T(8,128)(2,1)} %constant.6.clone.deriv_hbm.deriv_ref) | copy-start | bytes 786436

commit v5 on v4

--- a/solution.py
+++ b/solution.py
@@ -271,8 +271,8 @@
             axis=0,
         )
 
-    turned = gather(0) - mul((deriv_ref[0], deriv_ref[1]), halves(gather(1)))
-    lines = turned.T
+    slopes = mul(halves(gather(1).T), (deriv_ref[0], deriv_ref[1]), 1)
+    lines = gather(0).T - slopes
     for place in range(16):
         potential_ref[4 * (place // 4) + lax.rem(place % 4 + back, 4)] = lines[
             32 * place : 32 * (place + 1)

time: 59.1 us -> 59 us (level)
  no operation moved by 1% of the time
where the time goes in v5:
time: 59 us; the launch traced here: 58.8 us
  blocking collectives  52.7 us (89%)
  Pallas kernels  5.43 us (9%)
  between operations  0.66 us (1%)
    all_to_all x2, blocking collectives, exchange(): lax.all_to_all(values, ORDER, split_axis=0, concat_axis=0, tiled=True)  52.7 us
    pallas_call x1, Pallas kernels, body(): pl.pallas_call(middle_kernel, out_shape=jax.ShapeDtypeStruct((17 * LANES,...  2.61 us
    pallas_call x1, Pallas kernels, body(): pl.pallas_call(first_kernel, out_shape=jax.ShapeDtypeStruct((2048, LANES)...  1.59 us
    pallas_call x1, Pallas kernels, body(): pl.pallas_call(functools.partial(last_kernel, float(cells)), out_shape=(j...  1.22 us

profile of v5, /device:TPU:1, one launch (start us, length us, event | category | flops | bytes accessed | tf_op | source)
XLA Modules:
  0.0 58.8 jit_solution(13714102872645820019)
XLA Ops:
  0.6 1.6 %shard_map.59 = f32[2048,128]{1,0:T(8,128)S(1)} custom-call(f32[16,32,256]{2,1,0:T(8,128)} %density_hbm.1, bf16[2,256,256]{2,1,0:T(8,128)(2,1)} %constant.6.clone.deriv_hbm.deriv_ref), custom_call_target="tpu_custom_call" | custom-call | tf_op jit(solution)/shard_map/pallas_call | solution.py:314
  2.2 0.0 copy-start.1
  2.2 0.0 copy-start.2
  2.3 29.0 %all_to_all.10 = f32[128,16,128]{2,1,0:T(8,128)S(1)} all-to-all(f32[128,16,128]{2,1,0:T(8,128)S(1)} %bitcast.7), channel_id=1, replica_groups=mesh['z1'=2,'z0'=2,'yh'=2,'core'=2,'yl'=2,'x1'=2,'x0'=2] {'core','yh','y..., dimensions={0} | all-to-all | bytes 2097152 | tf_op jit(solution)/shard_map/all_to_all | solution.py:296
  31.3 0.0 copy-done.1
  31.3 0.0 copy-done.2
  31.3 2.6 %shard_map.60 = f32[2176,128]{1,0:T(8,128)S(1)} custom-call(f32[2048,128]{1,0:T(8,128)S(1)} %bitcast.8, bf16[2,256,256]{2,1,0:T(8,128)(2,1)S(1)} %copy-done.1, bf16[2,256,256]{2,1,0:T(8,128)(2,1)S(1)} %copy-done.2), custom_call_target="tpu_custom_call" | custom-call | tf_op jit(solution)/shard_map/pallas_call | solution.py:328
  33.9 0.0 copy-start
  33.9 23.7 %all_to_all.11 = f32[128,1,2176]{2,1,0:T(1,128)S(1)} all-to-all(f32[128,1,2176]{2,1,0:T(1,128)S(1)} %bitcast.6), channel_id=1, replica_groups=mesh['z1'=2,'z0'=2,'yh'=2,'core'=2,'yl'=2,'x1'=2,'x0'=2] {'core','yh','y..., dimensions={0} | all-to-all | bytes 2228224 | tf_op jit(solution)/shard_map/all_to_all | solution.py:296
  57.6 0.0 copy-done
  57.6 1.2 %shard_map.61 = (f32[16,32,256]{2,1,0:T(8,128)}, f32[1,1]{1,0:T(1,128)}) custom-call(f32[2176,128]{1,0:T(8,128)S(1)} %bitcast.5, bf16[2,256,256]{2,1,0:T(8,128)(2,1)S(1)} %copy-done), custom_call_target="tpu_custom_call" | custom-call | tf_op jit(solution)/shard_map/pallas_call | solution.py:337
Async XLA Ops:
  2.2 29.0 %copy-start.1 = (bf16[2,256,256]{2,1,0:T(8,128)(2,1)S(1)}, bf16[2,256,256]{2,1,0:T(8,128)(2,1)}, u32[]{:S(2)}) copy-start(bf16[2,256,256]{2,1,0:T(8,128)(2,1)} %constant.8.clone.deriv_x_ref) | copy-start | bytes 786436
  2.2 29.0 %copy-start.2 = (bf16[2,256,256]{2,1,0:T(8,128)(2,1)S(1)}, bf16[2,256,256]{2,1,0:T(8,128)(2,1)}, u32[]{:S(2)}) copy-start(bf16[2,256,256]{2,1,0:T(8,128)(2,1)} %constant.7.clone.deriv_y_ref) | copy-start | bytes 786436
  33.9 23.7 %copy-start = (bf16[2,256,256]{2,1,0:T(8,128)(2,1)S(1)}, bf16[2,256,256]{2,1,0:T(8,128)(2,1)}, u32[]{:S(2)}) copy-start(bf16[2,256,256]{2,1,0:T(8,128)(2,1)} %constant.6.clone.deriv_hbm.deriv_ref) | copy-start | bytes 786436

commit v6 on v5

--- a/solution.py
+++ b/solution.py
@@ -33,14 +33,17 @@
 s_scale = 1.0 / (4.0 * fermi_scale**2)
 t_scale = math.pi / (16.0 * fermi_scale)
 rs_scale = (3.0 / (4.0 * math.pi)) ** (1.0 / 3.0)
-ex_scale = -exch_scale / rs_scale**2
+stretch = (pbe_mu / pbe_kappa * s_scale / rs_scale**8) ** (1.0 / 16.0)
+ex_scale = -exch_scale / (rs_scale**2 * stretch**4)
 root_slope = -1.0 / (6.0 * math.log(2.0))
-root_shift = 0.5 * math.log2(rs_scale)
-damping_scale = pbe_mu / pbe_kappa * s_scale / rs_scale**8
-tau_scale = pbe_beta / pbe_gamma * t_scale / rs_scale**7
-slope_scale = -2.0 * exch_scale * s_scale * pbe_mu / rs_scale**4
-weight_scale = 2.0 * pbe_beta * t_scale / rs_scale**4
-pw = [2.0 * pw_coef * factor for factor in (pw_first, pw_second, pw_third, pw_fourth)]
+root_shift = 0.5 * math.log2(rs_scale) + math.log2(stretch)
+tau_scale = pbe_beta / pbe_gamma * t_scale / (rs_scale**7 * stretch**14)
+slope_scale = -2.0 * exch_scale * s_scale * pbe_mu / (rs_scale**4 * stretch**8)
+weight_scale = 2.0 * pbe_beta * t_scale / (rs_scale**4 * stretch**8)
+pw = [
+    2.0 * pw_coef * factor / stretch**power
+    for power, factor in enumerate((pw_first, pw_second, pw_third, pw_fourth), 1)
+]
 
 
 def deriv_matrix(count):
@@ -73,7 +76,7 @@
     rs2 = rs * rs
     rs4 = rs2 * rs2
     scaled = g * rs4
-    damping = 1.0 + damping_scale * (scaled * rs4)
+    damping = 1.0 + scaled * rs4
     tau = tau_scale * (scaled * (rs2 * rs))
     part = n * rs2
     series = root * (pw[0] + root * (pw[1] + root * (pw[2] + root * pw[3])))
@@ -84,7 +87,7 @@
     flipped = 1.0 / series
     fraction = flipped * (1.0 / (1.0 + series))
     logarithm = jnp.log(1.0 + flipped)
-    curved = (-2.0 * pw_coef * pw_alpha) * rs
+    curved = (-2.0 * pw_coef * pw_alpha / stretch**2) * rs
     front = curved - 2.0 * pw_coef
     ec = front * logarithm
     n_dec = front * (third * fraction) - (curved * (1.0 / 3.0)) * logarithm

time: 59 us -> 59 us (level)
  no operation moved by 1% of the time
where the time goes in v6:
time: 59 us; the launch traced here: 58.8 us
  blocking collectives  52.7 us (89%)
  Pallas kernels  5.43 us (9%)
  between operations  0.66 us (1%)
    all_to_all x2, blocking collectives, exchange(): lax.all_to_all(values, ORDER, split_axis=0, concat_axis=0, tiled=True)  52.7 us
    pallas_call x1, Pallas kernels, body(): pl.pallas_call(middle_kernel, out_shape=jax.ShapeDtypeStruct((17 * LANES,...  2.6 us
    pallas_call x1, Pallas kernels, body(): pl.pallas_call(first_kernel, out_shape=jax.ShapeDtypeStruct((2048, LANES)...  1.59 us
    pallas_call x1, Pallas kernels, body(): pl.pallas_call(functools.partial(last_kernel, float(cells)), out_shape=(j...  1.23 us

profile of v6, /device:TPU:1, one launch (start us, length us, event | category | flops | bytes accessed | tf_op | source)
XLA Modules:
  0.0 58.8 jit_solution(547071313430794733)
XLA Ops:
  0.6 1.6 %shard_map.59 = f32[2048,128]{1,0:T(8,128)S(1)} custom-call(f32[16,32,256]{2,1,0:T(8,128)} %density_hbm.1, bf16[2,256,256]{2,1,0:T(8,128)(2,1)} %constant.6.clone.deriv_hbm.deriv_ref), custom_call_target="tpu_custom_call" | custom-call | tf_op jit(solution)/shard_map/pallas_call | solution.py:317
  2.2 0.0 copy-start.1
  2.2 0.0 copy-start.2
  2.3 29.0 %all_to_all.10 = f32[128,16,128]{2,1,0:T(8,128)S(1)} all-to-all(f32[128,16,128]{2,1,0:T(8,128)S(1)} %bitcast.7), channel_id=1, replica_groups=mesh['z1'=2,'z0'=2,'yh'=2,'core'=2,'yl'=2,'x1'=2,'x0'=2] {'core','yh','y..., dimensions={0} | all-to-all | bytes 2097152 | tf_op jit(solution)/shard_map/all_to_all | solution.py:299
  31.3 0.0 copy-done.1
  31.3 0.0 copy-done.2
  31.3 2.6 %shard_map.60 = f32[2176,128]{1,0:T(8,128)S(1)} custom-call(f32[2048,128]{1,0:T(8,128)S(1)} %bitcast.8, bf16[2,256,256]{2,1,0:T(8,128)(2,1)S(1)} %copy-done.1, bf16[2,256,256]{2,1,0:T(8,128)(2,1)S(1)} %copy-done.2), custom_call_target="tpu_custom_call" | custom-call | tf_op jit(solution)/shard_map/pallas_call | solution.py:331
  33.9 0.0 copy-start
  33.9 23.7 %all_to_all.11 = f32[128,1,2176]{2,1,0:T(1,128)S(1)} all-to-all(f32[128,1,2176]{2,1,0:T(1,128)S(1)} %bitcast.6), channel_id=1, replica_groups=mesh['z1'=2,'z0'=2,'yh'=2,'core'=2,'yl'=2,'x1'=2,'x0'=2] {'core','yh','y..., dimensions={0} | all-to-all | bytes 2228224 | tf_op jit(solution)/shard_map/all_to_all | solution.py:299
  57.6 0.0 copy-done
  57.6 1.2 %shard_map.61 = (f32[16,32,256]{2,1,0:T(8,128)}, f32[1,1]{1,0:T(1,128)}) custom-call(f32[2176,128]{1,0:T(8,128)S(1)} %bitcast.5, bf16[2,256,256]{2,1,0:T(8,128)(2,1)S(1)} %copy-done), custom_call_target="tpu_custom_call" | custom-call | tf_op jit(solution)/shard_map/pallas_call | solution.py:340
Async XLA Ops:
  2.2 29.0 %copy-start.1 = (bf16[2,256,256]{2,1,0:T(8,128)(2,1)S(1)}, bf16[2,256,256]{2,1,0:T(8,128)(2,1)}, u32[]{:S(2)}) copy-start(bf16[2,256,256]{2,1,0:T(8,128)(2,1)} %constant.8.clone.deriv_x_ref) | copy-start | bytes 786436
  2.2 29.0 %copy-start.2 = (bf16[2,256,256]{2,1,0:T(8,128)(2,1)S(1)}, bf16[2,256,256]{2,1,0:T(8,128)(2,1)}, u32[]{:S(2)}) copy-start(bf16[2,256,256]{2,1,0:T(8,128)(2,1)} %constant.7.clone.deriv_y_ref) | copy-start | bytes 786436
  33.9 23.7 %copy-start = (bf16[2,256,256]{2,1,0:T(8,128)(2,1)S(1)}, bf16[2,256,256]{2,1,0:T(8,128)(2,1)}, u32[]{:S(2)}) copy-start(bf16[2,256,256]{2,1,0:T(8,128)(2,1)} %constant.6.clone.deriv_hbm.deriv_ref) | copy-start | bytes 786436
